TPU v7x, 32 devices: a whole 2x2x4 slice. The times are simulated.
32 devices in a mesh: dp: 4 (over x, core), ep: 8 (over z, y).
Axes of the slice: x: 2, y: 2, z: 4, core: 2. Of those that a mesh axis runs over, the one named last changes fastest.
Arguments:
- tokens: bfloat16 [4096, 2048], P(('dp', 'ep')), parts along dimension 0, may hold values from -6 to 6
- expert_ids: int32 [4096, 8], P(('dp', 'ep')), parts along dimension 0, may hold values from 0 to 15, all different within a row; in each aligned block of 32 rows (0 to 31, 32 to 63, ...) at most 32 rows name the same one
- gate_nums: int32 [4096, 8], P(('dp', 'ep')), parts along dimension 0, may hold values from 64 to 1023
- w_gate: bfloat16 [16, 2048, 768], P('ep'), may hold values from -0.125 to 0.125
- w_up: bfloat16 [16, 2048, 768], P('ep'), may hold values from -0.125 to 0.125
- w_down: bfloat16 [16, 768, 2048], P('ep'), may hold values from -0.21875 to 0.21875
Outputs:
- mixed: bfloat16 [4096, 2048], P(('dp', 'ep')), parts along dimension 0
There are 4 independent parts, one for each index of `dp`. A program takes and returns all parts, laid end to end along the dimension named above; an argument that names none is the same for every part. Nothing has to cross between parts.
Inputs may be any that keep to these rules, and one draw needn't show every extreme that they name: `expert_ids`: each row names 8 different experts. In every aligned block of 32 rows no expert is named by more than 32 rows, a bound that some block reaches.
All inputs are finite; a program needn't handle non-finite values.
Results may differ from a plain program's by a relative error of at most 0.008.
Values may be sent and summed in bfloat16 or wider, within the bound.
No kernel may reach another device: no remote copies, remote signals or barrier semaphores. Data moves between devices by JAX's collectives and lax.ppermute only.
A program may use at most 128 MiB of HBM per device.

v0:
```python
import jax
import jax.numpy as jnp
from jax import lax
from jax.sharding import PartitionSpec as P

TOP = 8
BLOCKS = 4


denominator = 1024.0


def shards(tokens, expert_ids, gate_nums, w_gate, w_up, w_down):
    ways = lax.axis_size("ep")
    local = w_gate.shape[0]
    experts = local * ways
    width = tokens.shape[1]
    block_rows = tokens.shape[0] // BLOCKS
    slots = 2 * block_rows * TOP // experts
    gates = gate_nums.astype(jnp.float32) / denominator
    labels = jnp.arange(experts, dtype=jnp.int32)
    slot_ids = jnp.arange(slots, dtype=jnp.int32)

    def expert_work(received):
        gate = jnp.einsum("sxcd,xdf->sxcf", received, w_gate, preferred_element_type=jnp.float32)
        up = jnp.einsum("sxcd,xdf->sxcf", received, w_up, preferred_element_type=jnp.float32)
        hidden = (jax.nn.silu(gate) * up).astype(jnp.bfloat16)
        result = jnp.einsum("sxcf,xfd->sxcd", hidden, w_down, preferred_element_type=jnp.float32)
        return lax.all_to_all(
            result.astype(jnp.bfloat16), "ep", split_axis=0, concat_axis=0, tiled=True
        )

    places = []
    weights = []
    buffers = []
    for block in range(BLOCKS):
        lower = block * block_rows
        ids_blk = expert_ids[lower : lower + block_rows]
        gates_blk = gates[lower : lower + block_rows]
        rows_blk = tokens[lower : lower + block_rows]
        onehot = ids_blk[:, :, None] == labels[None, None, :]
        member = jnp.sum(onehot.astype(jnp.int32), axis=1)
        before = jnp.cumsum(member, axis=0) - member
        place = (before[:, :, None] == slot_ids[None, None, :]) & (member[:, :, None] > 0)
        weight = jnp.sum(jnp.where(onehot, gates_blk[:, :, None], 0.0), axis=1)
        packed = jnp.einsum(
            "bec,bd->ecd", place.astype(jnp.bfloat16), rows_blk, preferred_element_type=jnp.float32
        )
        buffers.append(packed.astype(jnp.bfloat16).reshape(ways, local, slots, width))
        places.append(place)
        weights.append(weight)
    backs = [
        expert_work(lax.all_to_all(buffers[block], "ep", split_axis=0, concat_axis=0, tiled=True))
        for block in range(BLOCKS)
    ]
    outputs = []
    for block in range(BLOCKS):
        back = backs[block].reshape(experts, slots, width)
        mixing = jnp.where(places[block], weights[block][:, :, None], 0.0)
        high = mixing.astype(jnp.bfloat16)
        low = (mixing - high.astype(jnp.float32)).astype(jnp.bfloat16)
        part_high = jnp.einsum("bec,ecd->bd", high, back, preferred_element_type=jnp.float32)
        part_low = jnp.einsum("bec,ecd->bd", low, back, preferred_element_type=jnp.float32)
        outputs.append(part_high + part_low)
    return jnp.concatenate(outputs, axis=0).astype(jnp.bfloat16)


def solution(mesh):
    placed = (
        P(("dp", "ep"), None),
        P(("dp", "ep"), None),
        P(("dp", "ep"), None),
        P("ep", None, None),
        P("ep", None, None),
        P("ep", None, None),
    )
    return jax.shard_map(
        shards, mesh=mesh, in_specs=placed, out_specs=P(("dp", "ep"), None), check_vma=False
    )
```

profile of v0, /device:TPU:0, one launch (start us, length us, event | category | flops | bytes accessed | tf_op | source)
XLA Modules:
  0.0 430.7 jit_solution(11209908846326911032)
XLA Ops:
  1.2 3.3 convolution_convert_fusion.3
  4.4 7.4 %all-to-all-start = ((bf16[8,2,32,2048]{3,2,1,0:T(8,128)(2,1)}), bf16[8,2,32,2048]{3,2,1,0:T(8,128)(2,1)S(1)}, u32[]{:S(2)}, u32[]{:S(2)}) async-start(bf16[8,2,32,2048]{3,2,1,0:T(8,128)(2,1)} %bitcast.1), calls=%async_computation | async-start | bytes 4194304 | tf_op jit(solution)/shard_map/all_to_all | solution.py:53
  14.4 45.7 %all-to-all-done = bf16[8,2,32,2048]{3,2,1,0:T(8,128)(2,1)S(1)} async-done(((bf16[8,2,32,2048]{3,2,1,0:T(8,128)(2,1)}), bf16[8,2,32,2048]{3,2,1,0:T(8,128)(2,1)S(1)}, u32[]{:S(2)}, u32[]{:S(2)}) %all-to-all-start) | async-done | bytes 2097184 | tf_op jit(solution)/shard_map/all_to_all | solution.py:53
  60.1 4.3 %all-to-all-start.2 = ((bf16[8,2,32,2048]{3,2,1,0:T(8,128)(2,1)}), bf16[8,2,32,2048]{3,2,1,0:T(8,128)(2,1)}, u32[]{:S(2)}, u32[]{:S(2)}) async-start(bf16[8,2,32,2048]{3,2,1,0:T(8,128)(2,1)} %bitcast.15), calls=%async_computation.2 | async-start | bytes 4194304 | tf_op jit(solution)/shard_map/all_to_all | solution.py:53
  64.7 2.4 convolution_convert_fusion.1
  67.1 45.2 %all-to-all-done.2 = bf16[8,2,32,2048]{3,2,1,0:T(8,128)(2,1)} async-done(((bf16[8,2,32,2048]{3,2,1,0:T(8,128)(2,1)}), bf16[8,2,32,2048]{3,2,1,0:T(8,128)(2,1)}, u32[]{:S(2)}, u32[]{:S(2)}) %all-to-all-start.2) | async-done | bytes 2097184 | tf_op jit(solution)/shard_map/all_to_all | solution.py:53
  112.3 4.4 %all-to-all-start.4 = ((bf16[8,2,32,2048]{3,2,1,0:T(8,128)(2,1)}), bf16[8,2,32,2048]{3,2,1,0:T(8,128)(2,1)}, u32[]{:S(2)}, u32[]{:S(2)}) async-start(bf16[8,2,32,2048]{3,2,1,0:T(8,128)(2,1)} %bitcast.26), calls=%async_computation.4 | async-start | bytes 4194304 | tf_op jit(solution)/shard_map/all_to_all | solution.py:53
  116.9 2.4 convolution_convert_fusion
  119.3 45.1 %all-to-all-done.4 = bf16[8,2,32,2048]{3,2,1,0:T(8,128)(2,1)} async-done(((bf16[8,2,32,2048]{3,2,1,0:T(8,128)(2,1)}), bf16[8,2,32,2048]{3,2,1,0:T(8,128)(2,1)}, u32[]{:S(2)}, u32[]{:S(2)}) %all-to-all-start.4) | async-done | bytes 2097184 | tf_op jit(solution)/shard_map/all_to_all | solution.py:53
  164.5 4.3 %all-to-all-start.6 = ((bf16[8,2,32,2048]{3,2,1,0:T(8,128)(2,1)}), bf16[8,2,32,2048]{3,2,1,0:T(8,128)(2,1)}, u32[]{:S(2)}, u32[]{:S(2)}) async-start(bf16[8,2,32,2048]{3,2,1,0:T(8,128)(2,1)} %bitcast.34), calls=%async_computation.6 | async-start | bytes 4194304 | tf_op jit(solution)/shard_map/all_to_all | solution.py:53
  168.8 5.7 %fusion.22 = f32[2,8,32,768]{3,2,1,0:T(8,128)} fusion(bf16[2,2048,768]{2,1,0:T(8,128)(2,1)} %param.9, bf16[8,2,32,2048]{3,2,1,0:T(8,128)(2,1)S(1)} %all-to-all-done), kind=kOutput, calls=%fused_computation.22 | convolution fusion | flops 1610612736 | bytes 9961472 | tf_op jit(solution)/shard_map/sxcd,xdf->sxcf/dot_general | solution.py:25
  174.5 9.9 %fusion.45 = bf16[8,2,32,2048]{3,2,0,1:T(8,128)(2,1)} fusion(bf16[2,768,2048]{2,1,0:T(8,128)(2,1)} %param.11, f32[2,8,32,768]{3,2,1,0:T(8,128)} %fusion.22, bf16[2,2048,768]{2,1,0:T(8,128)(2,1)} %param.10, bf16[8,2,32,2048]{3,2,1,0:T(8,128)(2,1)S(1)} %all-to-all-done), kind=kOutput, calls=%fused_computation.35 | convolution fusion | flops 3224633344 | bytes 18350080 | tf_op jit(solution)/shard_map/sxcf,xfd->sxcd/dot_general | solution.py:28
  184.4 3.2 copy.97
  187.6 29.0 %all-to-all-done.6 = bf16[8,2,32,2048]{3,2,1,0:T(8,128)(2,1)} async-done(((bf16[8,2,32,2048]{3,2,1,0:T(8,128)(2,1)}), bf16[8,2,32,2048]{3,2,1,0:T(8,128)(2,1)}, u32[]{:S(2)}, u32[]{:S(2)}) %all-to-all-start.6) | async-done | bytes 2097184 | tf_op jit(solution)/shard_map/all_to_all | solution.py:53
  216.6 3.8 all-to-all-start.1
  220.4 6.4 %fusion.20 = f32[2,8,32,768]{3,2,1,0:T(8,128)} fusion(bf16[2,2048,768]{2,1,0:T(8,128)(2,1)} %param.9, bf16[8,2,32,2048]{3,2,1,0:T(8,128)(2,1)} %all-to-all-done.2), kind=kOutput, calls=%fused_computation.20 | convolution fusion | flops 1610612736 | bytes 9961472 | tf_op jit(solution)/shard_map/sxcd,xdf->sxcf/dot_general | solution.py:25
  226.9 10.5 %fusion.42 = bf16[8,2,32,2048]{3,2,0,1:T(8,128)(2,1)} fusion(bf16[2,768,2048]{2,1,0:T(8,128)(2,1)} %param.11, f32[2,8,32,768]{3,2,1,0:T(8,128)} %fusion.20, bf16[2,2048,768]{2,1,0:T(8,128)(2,1)} %param.10, bf16[8,2,32,2048]{3,2,1,0:T(8,128)(2,1)} %all-to-all-done.2), kind=kOutput, calls=%fused_computation.34 | convolution fusion | flops 3224633344 | bytes 18350080 | tf_op jit(solution)/shard_map/sxcf,xfd->sxcd/dot_general | solution.py:28
  237.3 3.2 copy.104
  240.6 28.2 %all-to-all-done.1 = bf16[8,2,32,2048]{3,2,1,0:T(8,128)(2,1)S(1)} async-done(((bf16[8,2,32,2048]{3,2,1,0:T(8,128)(2,1)}), bf16[8,2,32,2048]{3,2,1,0:T(8,128)(2,1)S(1)}, u32[]{:S(2)}, u32[]{:S(2)}) %all-to-all-start.1) | async-done | bytes 2097184 | tf_op jit(solution)/shard_map/all_to_all | solution.py:29
  268.7 4.3 %all-to-all-start.3 = ((bf16[8,2,32,2048]{3,2,1,0:T(8,128)(2,1)}), bf16[8,2,32,2048]{3,2,1,0:T(8,128)(2,1)}, u32[]{:S(2)}, u32[]{:S(2)}) async-start(bf16[8,2,32,2048]{3,2,1,0:T(8,128)(2,1)} %copy.104), calls=%async_computation.3 | async-start | bytes 4194304 | tf_op jit(solution)/shard_map/all_to_all | solution.py:29
  273.1 6.4 %fusion.18 = f32[2,8,32,768]{3,2,1,0:T(8,128)} fusion(bf16[2,2048,768]{2,1,0:T(8,128)(2,1)} %param.9, bf16[8,2,32,2048]{3,2,1,0:T(8,128)(2,1)} %all-to-all-done.4), kind=kOutput, calls=%fused_computation.18 | convolution fusion | flops 1610612736 | bytes 9961472 | tf_op jit(solution)/shard_map/sxcd,xdf->sxcf/dot_general | solution.py:25
  279.4 10.5 %fusion.39 = bf16[8,2,32,2048]{3,2,0,1:T(8,128)(2,1)} fusion(bf16[2,768,2048]{2,1,0:T(8,128)(2,1)} %param.11, f32[2,8,32,768]{3,2,1,0:T(8,128)} %fusion.18, bf16[2,2048,768]{2,1,0:T(8,128)(2,1)} %param.10, bf16[8,2,32,2048]{3,2,1,0:T(8,128)(2,1)} %all-to-all-done.4), kind=kOutput, calls=%fused_computation.33 | convolution fusion | flops 3224633344 | bytes 18350080 | tf_op jit(solution)/shard_map/sxcf,xfd->sxcd/dot_general | solution.py:28
  289.9 3.2 copy.111
  293.1 27.8 %all-to-all-done.3 = bf16[8,2,32,2048]{3,2,1,0:T(8,128)(2,1)} async-done(((bf16[8,2,32,2048]{3,2,1,0:T(8,128)(2,1)}), bf16[8,2,32,2048]{3,2,1,0:T(8,128)(2,1)}, u32[]{:S(2)}, u32[]{:S(2)}) %all-to-all-start.3) | async-done | bytes 2097184 | tf_op jit(solution)/shard_map/all_to_all | solution.py:29
  320.9 4.6 %all-to-all-start.5 = ((bf16[8,2,32,2048]{3,2,1,0:T(8,128)(2,1)}), bf16[8,2,32,2048]{3,2,1,0:T(8,128)(2,1)}, u32[]{:S(2)}, u32[]{:S(2)}) async-start(bf16[8,2,32,2048]{3,2,1,0:T(8,128)(2,1)} %copy.111), calls=%async_computation.5 | async-start | bytes 4194304 | tf_op jit(solution)/shard_map/all_to_all | solution.py:29
  325.5 6.4 %fusion.16 = f32[2,8,32,768]{3,2,1,0:T(8,128)} fusion(bf16[2,2048,768]{2,1,0:T(8,128)(2,1)} %param.9, bf16[8,2,32,2048]{3,2,1,0:T(8,128)(2,1)} %all-to-all-done.6), kind=kOutput, calls=%fused_computation.16 | convolution fusion | flops 1610612736 | bytes 9961472 | tf_op jit(solution)/shard_map/sxcd,xdf->sxcf/dot_general | solution.py:25
  331.8 10.6 %fusion.36 = bf16[8,2,32,2048]{3,2,0,1:T(8,128)(2,1)} fusion(bf16[2,768,2048]{2,1,0:T(8,128)(2,1)} %param.11, f32[2,8,32,768]{3,2,1,0:T(8,128)} %fusion.16, bf16[2,2048,768]{2,1,0:T(8,128)(2,1)} %param.10, bf16[8,2,32,2048]{3,2,1,0:T(8,128)(2,1)} %all-to-all-done.6), kind=kOutput, calls=%fused_computation.32 | convolution fusion | flops 3224633344 | bytes 18350080 | tf_op jit(solution)/shard_map/sxcf,xfd->sxcd/dot_general | solution.py:28
  342.4 3.2 copy.118
  345.6 27.6 %all-to-all-done.5 = bf16[8,2,32,2048]{3,2,1,0:T(8,128)(2,1)} async-done(((bf16[8,2,32,2048]{3,2,1,0:T(8,128)(2,1)}), bf16[8,2,32,2048]{3,2,1,0:T(8,128)(2,1)}, u32[]{:S(2)}, u32[]{:S(2)}) %all-to-all-start.5) | async-done | bytes 2097184 | tf_op jit(solution)/shard_map/all_to_all | solution.py:29
  373.1 4.4 %all-to-all-start.7 = ((bf16[8,2,32,2048]{3,2,1,0:T(8,128)(2,1)}), bf16[8,2,32,2048]{3,2,1,0:T(8,128)(2,1)}, u32[]{:S(2)}, u32[]{:S(2)}) async-start(bf16[8,2,32,2048]{3,2,1,0:T(8,128)(2,1)} %copy.118), calls=%async_computation.7 | async-start | bytes 4194304 | tf_op jit(solution)/shard_map/all_to_all | solution.py:29
  383.9 2.4 fusion.54
  388.6 36.6 %all-to-all-done.7 = bf16[8,2,32,2048]{3,2,1,0:T(8,128)(2,1)} async-done(((bf16[8,2,32,2048]{3,2,1,0:T(8,128)(2,1)}), bf16[8,2,32,2048]{3,2,1,0:T(8,128)(2,1)}, u32[]{:S(2)}, u32[]{:S(2)}) %all-to-all-start.7) | async-done | bytes 2097184 | tf_op jit(solution)/shard_map/all_to_all | solution.py:29
  (40 shorter events, 18.3 us)
Async XLA Ops:
  4.4 7.7 %copy-start = (bf16[128,2048]{1,0:T(8,128)(2,1)S(1)}, bf16[128,2048]{1,0:T(8,128)(2,1)}, u32[]{:S(2)}) copy-start(bf16[128,2048]{1,0:T(8,128)(2,1)} %param.6) | copy-start | bytes 1572868
  4.4 55.7 %all-to-all-start = ((bf16[8,2,32,2048]{3,2,1,0:T(8,128)(2,1)}), bf16[8,2,32,2048]{3,2,1,0:T(8,128)(2,1)S(1)}, u32[]{:S(2)}, u32[]{:S(2)}) async-start(bf16[8,2,32,2048]{3,2,1,0:T(8,128)(2,1)} %bitcast.1), calls=%async_computation | async-start | bytes 4194304 | tf_op jit(solution)/shard_map/all_to_all | solution.py:53
  60.1 52.2 %all-to-all-start.2 = ((bf16[8,2,32,2048]{3,2,1,0:T(8,128)(2,1)}), bf16[8,2,32,2048]{3,2,1,0:T(8,128)(2,1)}, u32[]{:S(2)}, u32[]{:S(2)}) async-start(bf16[8,2,32,2048]{3,2,1,0:T(8,128)(2,1)} %bitcast.15), calls=%async_computation.2 | async-start | bytes 4194304 | tf_op jit(solution)/shard_map/all_to_all | solution.py:53
  112.3 52.2 %all-to-all-start.4 = ((bf16[8,2,32,2048]{3,2,1,0:T(8,128)(2,1)}), bf16[8,2,32,2048]{3,2,1,0:T(8,128)(2,1)}, u32[]{:S(2)}, u32[]{:S(2)}) async-start(bf16[8,2,32,2048]{3,2,1,0:T(8,128)(2,1)} %bitcast.26), calls=%async_computation.4 | async-start | bytes 4194304 | tf_op jit(solution)/shard_map/all_to_all | solution.py:53
  164.5 52.2 %all-to-all-start.6 = ((bf16[8,2,32,2048]{3,2,1,0:T(8,128)(2,1)}), bf16[8,2,32,2048]{3,2,1,0:T(8,128)(2,1)}, u32[]{:S(2)}, u32[]{:S(2)}) async-start(bf16[8,2,32,2048]{3,2,1,0:T(8,128)(2,1)} %bitcast.34), calls=%async_computation.6 | async-start | bytes 4194304 | tf_op jit(solution)/shard_map/all_to_all | solution.py:53
  216.6 52.1 %all-to-all-start.1 = ((bf16[8,2,32,2048]{3,2,1,0:T(8,128)(2,1)}), bf16[8,2,32,2048]{3,2,1,0:T(8,128)(2,1)S(1)}, u32[]{:S(2)}, u32[]{:S(2)}) async-start(bf16[8,2,32,2048]{3,2,1,0:T(8,128)(2,1)} %copy.97), calls=%async_computation.1 | async-start | bytes 4194304 | tf_op jit(solution)/shard_map/all_to_all | solution.py:29
  268.7 52.1 %all-to-all-start.3 = ((bf16[8,2,32,2048]{3,2,1,0:T(8,128)(2,1)}), bf16[8,2,32,2048]{3,2,1,0:T(8,128)(2,1)}, u32[]{:S(2)}, u32[]{:S(2)}) async-start(bf16[8,2,32,2048]{3,2,1,0:T(8,128)(2,1)} %copy.104), calls=%async_computation.3 | async-start | bytes 4194304 | tf_op jit(solution)/shard_map/all_to_all | solution.py:29
  320.9 52.3 %all-to-all-start.5 = ((bf16[8,2,32,2048]{3,2,1,0:T(8,128)(2,1)}), bf16[8,2,32,2048]{3,2,1,0:T(8,128)(2,1)}, u32[]{:S(2)}, u32[]{:S(2)}) async-start(bf16[8,2,32,2048]{3,2,1,0:T(8,128)(2,1)} %copy.111), calls=%async_computation.5 | async-start | bytes 4194304 | tf_op jit(solution)/shard_map/all_to_all | solution.py:29
  345.6 31.9 %copy-start.1 = (s32[128,8]{0,1:T(8,128)S(1)}, s32[128,8]{0,1:T(8,128)}, u32[]{:S(2)}) copy-start(s32[128,8]{0,1:T(8,128)} %param.8) | copy-start | bytes 12292
  373.1 52.1 %all-to-all-start.7 = ((bf16[8,2,32,2048]{3,2,1,0:T(8,128)(2,1)}), bf16[8,2,32,2048]{3,2,1,0:T(8,128)(2,1)}, u32[]{:S(2)}, u32[]{:S(2)}) async-start(bf16[8,2,32,2048]{3,2,1,0:T(8,128)(2,1)} %copy.118), calls=%async_computation.7 | async-start | bytes 4194304 | tf_op jit(solution)/shard_map/all_to_all | solution.py:29
where the time goes:
time: 432 us; the launch traced here: 431 us
  waiting for transfers between devices  285 us (66%)
  matrix products  92.3 us (21%)
  starting transfers between devices  37.5 us (9%)
  local copies, waits for them, and re-layouts  14.4 us (3%)
    all_to_all x4, waiting for transfers between devices, shards(): lax.all_to_all(buffers[block], 'ep', split_axis=0, concat_axis=0, tiled=T...  165 us
    all_to_all x4, waiting for transfers between devices, expert_work(): lax.all_to_all(result.astype(jnp.bfloat16), 'ep', split_axis=0, concat_ax...  120 us
    dot_general x4, matrix products, expert_work(): jnp.einsum('sxcf,xfd->sxcd', hidden, w_down, preferred_element_type=jnp.f...  41.4 us
    dot_general x4, matrix products, expert_work(): jnp.einsum('sxcd,xdf->sxcf', received, w_gate, preferred_element_type=jnp...  24.9 us
    all_to_all x4, starting transfers between devices, shards(): lax.all_to_all(buffers[block], 'ep', split_axis=0, concat_axis=0, tiled=T...  20.5 us
    all_to_all x4, starting transfers between devices, expert_work(): lax.all_to_all(result.astype(jnp.bfloat16), 'ep', split_axis=0, concat_ax...  17.1 us
    convert_element_type x4, local copies, waits for them, and re-layouts, expert_work(): result.astype(jnp.bfloat16)  12.8 us
    dot_general x4, matrix products, shards(): jnp.einsum('bec,bd->ecd', place.astype(jnp.bfloat16), rows_blk, preferred...  10.5 us
  transfers between devices with their start and end apart: 8, of which 8 were waited for; matrix products, arithmetic and copies ran while one was open for 23% of the time, Pallas kernels for 0%

commit v1 on v0

--- a/solution.py
+++ b/solution.py
@@ -1,16 +1,21 @@
+import functools
+
 import jax
 import jax.numpy as jnp
 from jax import lax
+from jax.experimental import pallas as pl
+from jax.experimental.pallas import tpu as pltpu
 from jax.sharding import PartitionSpec as P
 
 TOP = 8
 BLOCKS = 4
+TILE = 256
 
 
 denominator = 1024.0
 
 
-def shards(tokens, expert_ids, gate_nums, w_gate, w_up, w_down):
+def packed_shards(tokens, expert_ids, gate_nums, w_gate, w_up, w_down):
     ways = lax.axis_size("ep")
     local = w_gate.shape[0]
     experts = local * ways
@@ -65,6 +70,121 @@
     return jnp.concatenate(outputs, axis=0).astype(jnp.bfloat16)
 
 
+def column(row):
+    n = row.shape[1]
+    square = lax.broadcasted_iota(jnp.int32, (n, n), 0) == lax.broadcasted_iota(
+        jnp.int32, (n, n), 1
+    )
+    return jnp.sum(jnp.where(square, jnp.broadcast_to(row, (n, n)), 0.0), axis=1, keepdims=True)
+
+
+def expert_kernel(a_ref, b_ref, scale_ref, wg_ref, wu_ref, wd_ref, oa_ref, ob_ref, x_ref, h_ref):
+    rows = a_ref.shape[0]
+    local, width, hidden = wg_ref.shape
+    x_ref[:rows] = a_ref[...]
+    x_ref[rows:] = b_ref[...]
+
+    for e in range(local):
+
+        @pl.loop(0, hidden // TILE)
+        def _(f):
+            cols = pl.ds(pl.multiple_of(f * TILE, TILE), TILE)
+            x = x_ref[...]
+            gate = jnp.dot(x, wg_ref[e, :, cols], preferred_element_type=jnp.float32)
+            up = jnp.dot(x, wu_ref[e, :, cols], preferred_element_type=jnp.float32)
+            h_ref[e, :, cols] = (jax.nn.silu(gate) * up).astype(jnp.bfloat16)
+
+    scales = [
+        jnp.concatenate([column(scale_ref[0, e : e + 1]), column(scale_ref[1, e : e + 1])], axis=0)
+        for e in range(local)
+    ]
+
+    @pl.loop(0, width // TILE)
+    def _(d):
+        cols = pl.ds(pl.multiple_of(d * TILE, TILE), TILE)
+        total = None
+        for e in range(local):
+            out = jnp.dot(h_ref[e], wd_ref[e, :, cols], preferred_element_type=jnp.float32)
+            term = out.astype(jnp.bfloat16).astype(jnp.float32) * scales[e]
+            total = term if total is None else total + term
+        total = total.astype(jnp.bfloat16)
+        oa_ref[:, cols] = total[:rows]
+        ob_ref[:, cols] = total[rows:]
+
+
+def expert_call(a, b, scale, w_gate, w_up, w_down):
+    rows, width = a.shape
+    local, _, hidden = w_gate.shape
+    in_vmem = pl.BlockSpec(memory_space=pltpu.VMEM)
+    held = [pltpu.with_memory_space_constraint(w, pltpu.VMEM) for w in (w_gate, w_up, w_down)]
+    out = jax.ShapeDtypeStruct((rows, width), jnp.bfloat16)
+    return pl.pallas_call(
+        expert_kernel,
+        out_shape=(out, out),
+        in_specs=[in_vmem] * 6,
+        out_specs=(in_vmem, in_vmem),
+        scratch_shapes=[
+            pltpu.VMEM((2 * rows, width), jnp.bfloat16),
+            pltpu.VMEM((local, 2 * rows, hidden), jnp.bfloat16),
+        ],
+        cost_estimate=pl.CostEstimate(
+            flops=2 * 2 * rows * local * width * hidden * 3,
+            bytes_accessed=4 * rows * width * 2,
+            transcendentals=2 * rows * local * hidden,
+        ),
+        compiler_params=pltpu.CompilerParams(vmem_limit_bytes=12 << 20),
+    )(a, b, scale, *held)
+
+
+def dense_shards(tokens, expert_ids, gate_nums, w_gate, w_up, w_down):
+    ways = lax.axis_size("ep")
+    local = w_gate.shape[0]
+    rows = tokens.shape[0]
+    planes = ways // 2
+    me = lax.axis_index("ep")
+    gates = gate_nums.astype(jnp.float32) / denominator
+    labels = jnp.arange(local * ways, dtype=jnp.int32)
+    hit = expert_ids.T[None, :, :] == labels[:, None, None]
+    weight = jnp.sum(jnp.where(hit, gates.T[None, :, :], 0.0), axis=1)
+    scales = lax.all_to_all(
+        weight.reshape(ways, local, rows), "ep", split_axis=0, concat_axis=0, tiled=True
+    )
+
+    def swap(array, offset):
+        return lax.ppermute(array, "ep", [(i, i ^ offset) for i in range(ways)])
+
+    order = [1, 3, 2] if planes == 4 else list(range(1, planes))
+    here = {0: tokens}
+    there = {0: swap(tokens, 1)}
+    for plane in order:
+        here[plane] = swap(tokens, 2 * plane)
+    for plane in order:
+        there[plane] = swap(here[plane], 1)
+
+    total = None
+    for plane in order + [0]:
+        source = me ^ (2 * plane)
+        pair = jnp.stack(
+            [
+                lax.dynamic_index_in_dim(scales, source, keepdims=False),
+                lax.dynamic_index_in_dim(scales, source ^ 1, keepdims=False),
+            ]
+        )
+        own, other = expert_call(here[plane], there[plane], pair, w_gate, w_up, w_down)
+        summed = own.astype(jnp.float32) + swap(other, 1).astype(jnp.float32)
+        if plane:
+            summed = swap(summed.astype(jnp.bfloat16), 2 * plane).astype(jnp.float32)
+        total = summed if total is None else total + summed
+    return total.astype(jnp.bfloat16)
+
+
+def shards(tokens, expert_ids, gate_nums, w_gate, w_up, w_down):
+    ways = lax.axis_size("ep")
+    dense = 2 * TOP >= w_gate.shape[0] * ways and ways & (ways - 1) == 0 and ways > 1
+    plan = dense_shards if dense else packed_shards
+    return plan(tokens, expert_ids, gate_nums, w_gate, w_up, w_down)
+
+
 def solution(mesh):
     placed = (
         P(("dp", "ep"), None),

time: 432 us -> 154 us (0.36)
  waiting for transfers between devices: 285 us -> 70.3 us
  matrix products: 92.3 us -> 0 us
  Pallas kernels: 0 us -> 31 us
  local copies, waits for them, and re-layouts: 14.4 us -> 9.41 us
    all_to_all x8 -> x1, waiting for transfers between devices: 285 us -> 25.8 us  [dense_shards(): lax.all_to_all(weight.reshape(ways, local, rows), 'ep', split_axis=0, con...]
    dot_general x20 -> x0, matrix products: 92.3 us -> none  [the longest x4 41.4 us: expert_work(): jnp.einsum('sxcf,xfd->sxcd', hidden, w_down, preferred_element_type=jnp.f...]
    ppermute x0 -> x14, waiting for transfers between devices: none -> 44.6 us  [swap(): return lax.ppermute(array, 'ep', [(i, i ^ offset) for i in range(ways)])]
    ppermute x0 -> x14, starting transfers between devices: none -> 35.3 us  [swap(): return lax.ppermute(array, 'ep', [(i, i ^ offset) for i in range(ways)])]
    all_to_all x8 -> x1, starting transfers between devices: 37.5 us -> 3.81 us  [dense_shards(): lax.all_to_all(weight.reshape(ways, local, rows), 'ep', split_axis=0, con...]
    pallas_call x0 -> x4, Pallas kernels: none -> 31 us  [expert_call(): pl.pallas_call(expert_kernel, out_shape=(out, out), in_specs=[in_vmem] *...]
    convert_element_type x4 -> x0, local copies, waits for them, and re-layouts: 12.8 us -> none  [expert_work(): result.astype(jnp.bfloat16)]
    unnamed x4 -> x14, local copies, waits for them, and re-layouts: 0.01 us -> 9.41 us
  transfers between devices with their start and end apart: 8 -> 15, of which waited for: 8 -> 7; matrix products, arithmetic and copies ran while one was open for 23% -> 2% of each run, Pallas kernels for 0% -> 20%
where the time goes in v1:
time: 154 us
  waiting for transfers between devices  70.3 us (46%)
  starting transfers between devices  39.1 us (25%)
  Pallas kernels  31 us (20%)
  local copies, waits for them, and re-layouts  9.41 us (6%)
  other arithmetic  3.62 us (2%)
    ppermute x14, waiting for transfers between devices, swap(): return lax.ppermute(array, 'ep', [(i, i ^ offset) for i in range(ways)])  44.6 us
    ppermute x14, starting transfers between devices, swap(): return lax.ppermute(array, 'ep', [(i, i ^ offset) for i in range(ways)])  35.3 us
    pallas_call x4, Pallas kernels, expert_call(): pl.pallas_call(expert_kernel, out_shape=(out, out), in_specs=[in_vmem] *...  31 us
    all_to_all x1, waiting for transfers between devices, dense_shards(): lax.all_to_all(weight.reshape(ways, local, rows), 'ep', split_axis=0, con...  25.8 us
    unnamed x14, local copies, waits for them, and re-layouts  9.41 us
    all_to_all x1, starting transfers between devices, dense_shards(): lax.all_to_all(weight.reshape(ways, local, rows), 'ep', split_axis=0, con...  3.81 us
  transfers between devices with their start and end apart: 15, of which 7 were waited for; matrix products, arithmetic and copies ran while one was open for 2% of the time, Pallas kernels for 20%

profile of v1, /device:TPU:0, one launch (start us, length us, event | category | flops | bytes accessed | tf_op | source)
XLA Modules:
  0.0 153.6 jit_solution(1877748937782388792)
XLA Ops:
  0.0 4.1 %collective-permute-start.8 = (bf16[128,2048]{1,0:T(8,128)(2,1)}, bf16[128,2048]{1,0:T(8,128)(2,1)S(1)}, u32[]{:S(2)}, u32[]{:S(2)}) collective-permute-start(bf16[128,2048]{1,0:T(8,128)(2,1)} %a_ref.1), channel_id=1, source_target_pairs={{0,4},{1,5},{2,6},{3,7},{4,0},{5,1},{6,2},{7,3},{8,12},{9,13},{10,... | collective-permute-start | bytes 1572872 | tf_op jit(solution)/shard_map/ppermute | solution.py:154
  4.1 0.7 multiply_bitcast_fusion
  4.8 1.3 select_reduce_fusion
  6.1 3.8 %all-to-all-start = ((f32[8,2,128]{2,1,0:T(2,128)}), f32[8,2,128]{2,1,0:T(2,128)S(1)}, u32[]{:S(2)}, u32[]{:S(2)}) async-start(f32[8,2,128]{2,1,0:T(2,128)} %bitcast.2), calls=%async_computation | async-start | bytes 16384 | tf_op jit(solution)/shard_map/all_to_all | solution.py:149
  9.9 3.8 %collective-permute-start.4 = (bf16[128,2048]{1,0:T(8,128)(2,1)}, bf16[128,2048]{1,0:T(8,128)(2,1)S(1)}, u32[]{:S(2)}, u32[]{:S(2)}) collective-permute-start(bf16[128,2048]{1,0:T(8,128)(2,1)} %a_ref.1), channel_id=1, source_target_pairs={{0,6},{1,7},{2,4},{3,5},{4,2},{5,3},{6,0},{7,1},{8,14},{9,15},{10,... | collective-permute-start | bytes 1572872 | tf_op jit(solution)/shard_map/ppermute | solution.py:154
  13.7 1.5 collective-permute-start.12
  15.2 25.8 %all-to-all-done = f32[8,2,128]{2,1,0:T(2,128)S(1)} async-done(((f32[8,2,128]{2,1,0:T(2,128)}), f32[8,2,128]{2,1,0:T(2,128)S(1)}, u32[]{:S(2)}, u32[]{:S(2)}) %all-to-all-start) | async-done | bytes 8224 | tf_op jit(solution)/shard_map/all_to_all | solution.py:149
  41.0 0.7 collective-permute-start.9
  41.7 1.4 collective-permute-start.5
  43.1 2.8 %copy-done = bf16[2,2048,768]{2,1,0:T(8,128)(2,1)S(1)} copy-done((bf16[2,2048,768]{2,1,0:T(8,128)(2,1)S(1)}, bf16[2,2048,768]{2,1,0:T(8,128)(2,1)}, u32[]{:S(2)}) %copy-start) | copy-done | bytes 6291480
  45.9 2.8 %copy-done.2 = bf16[2,2048,768]{2,1,0:T(8,128)(2,1)S(1)} copy-done((bf16[2,2048,768]{2,1,0:T(8,128)(2,1)S(1)}, bf16[2,2048,768]{2,1,0:T(8,128)(2,1)}, u32[]{:S(2)}) %copy-start.2) | copy-done | bytes 6291480
  48.7 2.8 %copy-done.4 = bf16[2,768,2048]{2,1,0:T(8,128)(2,1)S(1)} copy-done((bf16[2,768,2048]{2,1,0:T(8,128)(2,1)S(1)}, bf16[2,768,2048]{2,1,0:T(8,128)(2,1)}, u32[]{:S(2)}) %copy-start.4) | copy-done | bytes 6291480
  51.5 1.0 copy-done.6
  52.5 7.8 %shard_map.67 = (bf16[128,2048]{1,0:T(8,128)(2,1)S(1)}, bf16[128,2048]{1,0:T(8,128)(2,1)S(1)}) custom-call(bf16[128,2048]{1,0:T(8,128)(2,1)S(1)} %copy-done.6, bf16[128,2048]{1,0:T(8,128)(2,1)S(1)} %collective-permute-done.12.b_ref, f32[2,2,128]{2,1,0:T(2,128)S(1)} %pad_maximum_fusion.3.scale_ref, bf16[2,2048,768]{2,1,0:T(8,128)(2,1)S(1)} %copy-done, ...), custom_call_target="tpu_custom_call" | custom-call | flops 4831838208 | bytes 2097152 | tf_op jit(solution)/shard_map/pallas_call | solution.py:121
  60.3 0.7 collective-permute-start.13
  61.0 1.4 collective-permute-start.1
  62.4 7.8 %shard_map.66 = (bf16[128,2048]{1,0:T(8,128)(2,1)S(1)}, bf16[128,2048]{1,0:T(8,128)(2,1)S(1)}) custom-call(bf16[128,2048]{1,0:T(8,128)(2,1)S(1)} %collective-permute-done.8.a_ref, bf16[128,2048]{1,0:T(8,128)(2,1)S(1)} %collective-permute-done.9.b_ref, f32[2,2,128]{2,1,0:T(2,128)S(1)} %pad_maximum_fusion.2.scale_ref, bf16[2,2048,768]{2,1,0:T(8,128)(2,1)S(1)} %copy-done.1, ...), custom_call_target="tpu_custom_call" | custom-call | flops 4831838208 | bytes 2097152 | tf_op jit(solution)/shard_map/pallas_call | solution.py:121
  70.2 0.7 collective-permute-start.10
  70.8 7.8 %shard_map.65 = (bf16[128,2048]{1,0:T(8,128)(2,1)S(1)}, bf16[128,2048]{1,0:T(8,128)(2,1)S(1)}) custom-call(bf16[128,2048]{1,0:T(8,128)(2,1)S(1)} %collective-permute-done.4.a_ref, bf16[128,2048]{1,0:T(8,128)(2,1)S(1)} %collective-permute-done.5.b_ref, f32[2,2,128]{2,1,0:T(2,128)S(1)} %pad_maximum_fusion.1.scale_ref, bf16[2,2048,768]{2,1,0:T(8,128)(2,1)S(1)} %copy-done.1, ...), custom_call_target="tpu_custom_call" | custom-call | flops 4831838208 | bytes 2097152 | tf_op jit(solution)/shard_map/pallas_call | solution.py:121
  78.6 1.5 collective-permute-start.6
  80.1 9.5 %collective-permute-done.1.b_ref = bf16[128,2048]{1,0:T(8,128)(2,1)S(1)} collective-permute-done((bf16[128,2048]{1,0:T(8,128)(2,1)S(1)}, bf16[128,2048]{1,0:T(8,128)(2,1)S(1)}, u32[]{:S(2)}, u32[]{:S(2)}) %collective-permute-start.1) | collective-permute-done | bytes 524320 | tf_op jit(solution)/shard_map/ppermute | solution.py:154
  89.6 7.8 %shard_map.64 = (bf16[128,2048]{1,0:T(8,128)(2,1)S(1)}, bf16[128,2048]{1,0:T(8,128)(2,1)S(1)}) custom-call(bf16[128,2048]{1,0:T(8,128)(2,1)S(1)} %collective-permute-done.a_ref, bf16[128,2048]{1,0:T(8,128)(2,1)S(1)} %collective-permute-done.1.b_ref, f32[2,2,128]{2,1,0:T(2,128)S(1)} %pad_maximum_fusion.scale_ref, bf16[2,2048,768]{2,1,0:T(8,128)(2,1)S(1)} %copy-done.1, ...), custom_call_target="tpu_custom_call" | custom-call | flops 4831838208 | bytes 2097152 | tf_op jit(solution)/shard_map/pallas_call | solution.py:121
  97.3 0.7 collective-permute-start.2
  98.0 2.8 %collective-permute-done.10 = bf16[128,2048]{1,0:T(8,128)(2,1)S(1)} collective-permute-done((bf16[128,2048]{1,0:T(8,128)(2,1)S(1)}, bf16[128,2048]{1,0:T(8,128)(2,1)S(1)}, u32[]{:S(2)}, u32[]{:S(2)}) %collective-permute-start.10) | collective-permute-done | bytes 524320 | tf_op jit(solution)/shard_map/ppermute | solution.py:154
  100.9 8.1 %collective-permute-start.11 = (bf16[128,2048]{1,0:T(8,128)(2,1)S(1)}, bf16[128,2048]{1,0:T(8,128)(2,1)S(1)}, u32[]{:S(2)}, u32[]{:S(2)}) collective-permute-start(bf16[128,2048]{1,0:T(8,128)(2,1)S(1)} %add_convert_fusion.1), channel_id=1, source_target_pairs={{0,4},{1,5},{2,6},{3,7},{4,0},{5,1},{6,2},{7,3},{8,12},{9,13},{10,... | collective-permute-start | bytes 1572872 | tf_op jit(solution)/shard_map/ppermute | solution.py:154
  109.0 3.0 %collective-permute-done.6 = bf16[128,2048]{1,0:T(8,128)(2,1)S(1)} collective-permute-done((bf16[128,2048]{1,0:T(8,128)(2,1)S(1)}, bf16[128,2048]{1,0:T(8,128)(2,1)S(1)}, u32[]{:S(2)}, u32[]{:S(2)}) %collective-permute-start.6) | collective-permute-done | bytes 524320 | tf_op jit(solution)/shard_map/ppermute | solution.py:154
  112.2 2.5 %collective-permute-start.7 = (bf16[128,2048]{1,0:T(8,128)(2,1)S(1)}, bf16[128,2048]{1,0:T(8,128)(2,1)S(1)}, u32[]{:S(2)}, u32[]{:S(2)}) collective-permute-start(bf16[128,2048]{1,0:T(8,128)(2,1)S(1)} %add_convert_fusion.2), channel_id=1, source_target_pairs={{0,6},{1,7},{2,4},{3,5},{4,2},{5,3},{6,0},{7,1},{8,14},{9,15},{10,... | collective-permute-start | bytes 1572872 | tf_op jit(solution)/shard_map/ppermute | solution.py:154
  114.7 5.2 %collective-permute-done.2 = bf16[128,2048]{1,0:T(8,128)(2,1)S(1)} collective-permute-done((bf16[128,2048]{1,0:T(8,128)(2,1)S(1)}, bf16[128,2048]{1,0:T(8,128)(2,1)S(1)}, u32[]{:S(2)}, u32[]{:S(2)}) %collective-permute-start.2) | collective-permute-done | bytes 524320 | tf_op jit(solution)/shard_map/ppermute | solution.py:154
  120.1 8.3 %collective-permute-start.3 = (bf16[128,2048]{1,0:T(8,128)(2,1)S(1)}, bf16[128,2048]{1,0:T(8,128)(2,1)S(1)}, u32[]{:S(2)}, u32[]{:S(2)}) collective-permute-start(bf16[128,2048]{1,0:T(8,128)(2,1)S(1)} %add_convert_fusion.3), channel_id=1, source_target_pairs={{0,2},{1,3},{2,0},{3,1},{4,6},{5,7},{6,4},{7,5},{8,10},{9,11},{10,... | collective-permute-start | bytes 1572872 | tf_op jit(solution)/shard_map/ppermute | solution.py:154
  128.4 13.2 %collective-permute-done.11 = bf16[128,2048]{1,0:T(8,128)(2,1)S(1)} collective-permute-done((bf16[128,2048]{1,0:T(8,128)(2,1)S(1)}, bf16[128,2048]{1,0:T(8,128)(2,1)S(1)}, u32[]{:S(2)}, u32[]{:S(2)}) %collective-permute-start.11) | collective-permute-done | bytes 524320 | tf_op jit(solution)/shard_map/ppermute | solution.py:154
  141.6 10.8 %collective-permute-done.3 = bf16[128,2048]{1,0:T(8,128)(2,1)S(1)} collective-permute-done((bf16[128,2048]{1,0:T(8,128)(2,1)S(1)}, bf16[128,2048]{1,0:T(8,128)(2,1)S(1)}, u32[]{:S(2)}, u32[]{:S(2)}) %collective-permute-start.3) | collective-permute-done | bytes 524320 | tf_op jit(solution)/shard_map/ppermute | solution.py:154
  152.4 1.2 add_convert_fusion
  (27 shorter events, 0.5 us)
Async XLA Ops:
  0.0 41.0 %collective-permute-start.8 = (bf16[128,2048]{1,0:T(8,128)(2,1)}, bf16[128,2048]{1,0:T(8,128)(2,1)S(1)}, u32[]{:S(2)}, u32[]{:S(2)}) collective-permute-start(bf16[128,2048]{1,0:T(8,128)(2,1)} %a_ref.1), channel_id=1, source_target_pairs={{0,4},{1,5},{2,6},{3,7},{4,0},{5,1},{6,2},{7,3},{8,12},{9,13},{10,... | collective-permute-start | bytes 1572872 | tf_op jit(solution)/shard_map/ppermute | solution.py:154
  6.1 34.9 %all-to-all-start = ((f32[8,2,128]{2,1,0:T(2,128)}), f32[8,2,128]{2,1,0:T(2,128)S(1)}, u32[]{:S(2)}, u32[]{:S(2)}) async-start(f32[8,2,128]{2,1,0:T(2,128)} %bitcast.2), calls=%async_computation | async-start | bytes 16384 | tf_op jit(solution)/shard_map/all_to_all | solution.py:149
  9.9 31.8 %collective-permute-start.4 = (bf16[128,2048]{1,0:T(8,128)(2,1)}, bf16[128,2048]{1,0:T(8,128)(2,1)S(1)}, u32[]{:S(2)}, u32[]{:S(2)}) collective-permute-start(bf16[128,2048]{1,0:T(8,128)(2,1)} %a_ref.1), channel_id=1, source_target_pairs={{0,6},{1,7},{2,4},{3,5},{4,2},{5,3},{6,0},{7,1},{8,14},{9,15},{10,... | collective-permute-start | bytes 1572872 | tf_op jit(solution)/shard_map/ppermute | solution.py:154
  13.7 47.3 %collective-permute-start = (bf16[128,2048]{1,0:T(8,128)(2,1)}, bf16[128,2048]{1,0:T(8,128)(2,1)S(1)}, u32[]{:S(2)}, u32[]{:S(2)}) collective-permute-start(bf16[128,2048]{1,0:T(8,128)(2,1)} %a_ref.1), channel_id=1, source_target_pairs={{0,2},{1,3},{2,0},{3,1},{4,6},{5,7},{6,4},{7,5},{8,10},{9,11},{10,... | collective-permute-start | bytes 1572872 | tf_op jit(solution)/shard_map/ppermute | solution.py:154
  13.7 29.4 %collective-permute-start.12 = (bf16[128,2048]{1,0:T(8,128)(2,1)}, bf16[128,2048]{1,0:T(8,128)(2,1)S(1)}, u32[]{:S(2)}, u32[]{:S(2)}) collective-permute-start(bf16[128,2048]{1,0:T(8,128)(2,1)} %a_ref.1), channel_id=1, source_target_pairs={{0,1},{1,0},{2,3},{3,2},{4,5},{5,4},{6,7},{7,6},{8,9},{9,8},{10,11... | collective-permute-start | bytes 1572872 | tf_op jit(solution)/shard_map/ppermute | solution.py:154
  41.0 21.4 %collective-permute-start.9 = (bf16[128,2048]{1,0:T(8,128)(2,1)S(1)}, bf16[128,2048]{1,0:T(8,128)(2,1)S(1)}, u32[]{:S(2)}, u32[]{:S(2)}) collective-permute-start(bf16[128,2048]{1,0:T(8,128)(2,1)S(1)} %collective-permute-done.8.a_ref), channel_id=1, source_target_pairs={{0,1},{1,0},{2,3},{3,2},{4,5},{5,4},{6,7},{7,6},{8,9},{9,8},{10,11... | collective-permute-start | bytes 1572872 | tf_op jit(solution)/shard_map/ppermute | solution.py:154
  41.7 29.2 %collective-permute-start.5 = (bf16[128,2048]{1,0:T(8,128)(2,1)S(1)}, bf16[128,2048]{1,0:T(8,128)(2,1)S(1)}, u32[]{:S(2)}, u32[]{:S(2)}) collective-permute-start(bf16[128,2048]{1,0:T(8,128)(2,1)S(1)} %collective-permute-done.4.a_ref), channel_id=1, source_target_pairs={{0,1},{1,0},{2,3},{3,2},{4,5},{5,4},{6,7},{7,6},{8,9},{9,8},{10,11... | collective-permute-start | bytes 1572872 | tf_op jit(solution)/shard_map/ppermute | solution.py:154
  43.1 2.8 %copy-start = (bf16[2,2048,768]{2,1,0:T(8,128)(2,1)S(1)}, bf16[2,2048,768]{2,1,0:T(8,128)(2,1)}, u32[]{:S(2)}) copy-start(bf16[2,2048,768]{2,1,0:T(8,128)(2,1)} %wg_ref.7) | copy-start | bytes 18874372
  45.9 2.8 %copy-start.2 = (bf16[2,2048,768]{2,1,0:T(8,128)(2,1)S(1)}, bf16[2,2048,768]{2,1,0:T(8,128)(2,1)}, u32[]{:S(2)}) copy-start(bf16[2,2048,768]{2,1,0:T(8,128)(2,1)} %wu_ref.7) | copy-start | bytes 18874372
  48.7 2.8 %copy-start.4 = (bf16[2,768,2048]{2,1,0:T(8,128)(2,1)S(1)}, bf16[2,768,2048]{2,1,0:T(8,128)(2,1)}, u32[]{:S(2)}) copy-start(bf16[2,768,2048]{2,1,0:T(8,128)(2,1)} %wd_ref.7) | copy-start | bytes 18874372
  51.5 1.0 copy-start.6
  52.5 9.9 %copy-start.1 = (bf16[2,2048,768]{2,1,0:T(8,128)(2,1)S(1)}, bf16[2,2048,768]{2,1,0:T(8,128)(2,1)}, u32[]{:S(2)}) copy-start(bf16[2,2048,768]{2,1,0:T(8,128)(2,1)} %wg_ref.7) | copy-start | bytes 18874372
  52.5 9.9 %copy-start.3 = (bf16[2,2048,768]{2,1,0:T(8,128)(2,1)S(1)}, bf16[2,2048,768]{2,1,0:T(8,128)(2,1)}, u32[]{:S(2)}) copy-start(bf16[2,2048,768]{2,1,0:T(8,128)(2,1)} %wu_ref.7) | copy-start | bytes 18874372
  52.5 9.9 %copy-start.5 = (bf16[2,768,2048]{2,1,0:T(8,128)(2,1)S(1)}, bf16[2,768,2048]{2,1,0:T(8,128)(2,1)}, u32[]{:S(2)}) copy-start(bf16[2,768,2048]{2,1,0:T(8,128)(2,1)} %wd_ref.7) | copy-start | bytes 18874372
  60.3 68.1 %collective-permute-start.13 = (bf16[128,2048]{1,0:T(8,128)(2,1)S(1)}, bf16[128,2048]{1,0:T(8,128)(2,1)S(1)}, u32[]{:S(2)}, u32[]{:S(2)}) collective-permute-start(bf16[128,2048]{1,0:T(8,128)(2,1)S(1)} %get-tuple-element.20), channel_id=1, source_target_pairs={{0,1},{1,0},{2,3},{3,2},{4,5},{5,4},{6,7},{7,6},{8,9},{9,8},{10,11... | collective-permute-start | bytes 1572872 | tf_op jit(solution)/shard_map/ppermute | solution.py:154
  61.0 28.6 %collective-permute-start.1 = (bf16[128,2048]{1,0:T(8,128)(2,1)S(1)}, bf16[128,2048]{1,0:T(8,128)(2,1)S(1)}, u32[]{:S(2)}, u32[]{:S(2)}) collective-permute-start(bf16[128,2048]{1,0:T(8,128)(2,1)S(1)} %collective-permute-done.a_ref), channel_id=1, source_target_pairs={{0,1},{1,0},{2,3},{3,2},{4,5},{5,4},{6,7},{7,6},{8,9},{9,8},{10,11... | collective-permute-start | bytes 1572872 | tf_op jit(solution)/shard_map/ppermute | solution.py:154
  70.2 30.6 %collective-permute-start.10 = (bf16[128,2048]{1,0:T(8,128)(2,1)S(1)}, bf16[128,2048]{1,0:T(8,128)(2,1)S(1)}, u32[]{:S(2)}, u32[]{:S(2)}) collective-permute-start(bf16[128,2048]{1,0:T(8,128)(2,1)S(1)} %get-tuple-element.18), channel_id=1, source_target_pairs={{0,1},{1,0},{2,3},{3,2},{4,5},{5,4},{6,7},{7,6},{8,9},{9,8},{10,11... | collective-permute-start | bytes 1572872 | tf_op jit(solution)/shard_map/ppermute | solution.py:154
  78.6 33.4 %collective-permute-start.6 = (bf16[128,2048]{1,0:T(8,128)(2,1)S(1)}, bf16[128,2048]{1,0:T(8,128)(2,1)S(1)}, u32[]{:S(2)}, u32[]{:S(2)}) collective-permute-start(bf16[128,2048]{1,0:T(8,128)(2,1)S(1)} %get-tuple-element.16), channel_id=1, source_target_pairs={{0,1},{1,0},{2,3},{3,2},{4,5},{5,4},{6,7},{7,6},{8,9},{9,8},{10,11... | collective-permute-start | bytes 1572872 | tf_op jit(solution)/shard_map/ppermute | solution.py:154
  97.3 22.6 %collective-permute-start.2 = (bf16[128,2048]{1,0:T(8,128)(2,1)S(1)}, bf16[128,2048]{1,0:T(8,128)(2,1)S(1)}, u32[]{:S(2)}, u32[]{:S(2)}) collective-permute-start(bf16[128,2048]{1,0:T(8,128)(2,1)S(1)} %get-tuple-element.14), channel_id=1, source_target_pairs={{0,1},{1,0},{2,3},{3,2},{4,5},{5,4},{6,7},{7,6},{8,9},{9,8},{10,11... | collective-permute-start | bytes 1572872 | tf_op jit(solution)/shard_map/ppermute | solution.py:154
  100.9 40.7 %collective-permute-start.11 = (bf16[128,2048]{1,0:T(8,128)(2,1)S(1)}, bf16[128,2048]{1,0:T(8,128)(2,1)S(1)}, u32[]{:S(2)}, u32[]{:S(2)}) collective-permute-start(bf16[128,2048]{1,0:T(8,128)(2,1)S(1)} %add_convert_fusion.1), channel_id=1, source_target_pairs={{0,4},{1,5},{2,6},{3,7},{4,0},{5,1},{6,2},{7,3},{8,12},{9,13},{10,... | collective-permute-start | bytes 1572872 | tf_op jit(solution)/shard_map/ppermute | solution.py:154
  112.2 29.4 %collective-permute-start.7 = (bf16[128,2048]{1,0:T(8,128)(2,1)S(1)}, bf16[128,2048]{1,0:T(8,128)(2,1)S(1)}, u32[]{:S(2)}, u32[]{:S(2)}) collective-permute-start(bf16[128,2048]{1,0:T(8,128)(2,1)S(1)} %add_convert_fusion.2), channel_id=1, source_target_pairs={{0,6},{1,7},{2,4},{3,5},{4,2},{5,3},{6,0},{7,1},{8,14},{9,15},{10,... | collective-permute-start | bytes 1572872 | tf_op jit(solution)/shard_map/ppermute | solution.py:154
  120.1 32.3 %collective-permute-start.3 = (bf16[128,2048]{1,0:T(8,128)(2,1)S(1)}, bf16[128,2048]{1,0:T(8,128)(2,1)S(1)}, u32[]{:S(2)}, u32[]{:S(2)}) collective-permute-start(bf16[128,2048]{1,0:T(8,128)(2,1)S(1)} %add_convert_fusion.3), channel_id=1, source_target_pairs={{0,2},{1,3},{2,0},{3,1},{4,6},{5,7},{6,4},{7,5},{8,10},{9,11},{10,... | collective-permute-start | bytes 1572872 | tf_op jit(solution)/shard_map/ppermute | solution.py:154
